TPU v7x, 32 devices: a whole 2x2x4 slice. The times are simulated.
32 devices in a mesh: aux: 4 (over x, core), row: 8 (over z, y).
Axes of the slice: x: 2, y: 2, z: 4, core: 2. Of those that a mesh axis runs over, the one named last changes fastest.
Arguments:
- integrals: bfloat16 [4, 8192, 8192], P('aux', 'row'), may hold values from -6 to 6
- orbitals: bfloat16 [8192, 768], P('row'), may hold values from -0.0011901855 to 0.0011901855
Outputs:
- exchange_matrix: float32 [8192, 8192], P('row', 'aux')
All inputs are finite; a program needn't handle non-finite values.
Results may differ from a plain program's by a relative error of at most 0.0033.
Values may be sent and summed in bfloat16 or wider, within the bound.
A program may use at most 128 MiB of HBM per device.

v0:
```python
import jax
import jax.numpy as jnp
from jax import lax
from jax.sharding import PartitionSpec as P


def block_product(own_block, other_block):
    return jnp.einsum("aro,aso->rs", own_block, other_block, preferred_element_type=jnp.float32)


def body(integrals, orbitals):
    transformed = jnp.einsum(
        "arn,no->aro",
        integrals,
        lax.all_gather(orbitals, "row", axis=0, tiled=True),
        preferred_element_type=jnp.float32,
    )
    own_half = transformed.astype(jnp.bfloat16)
    partial_k = block_product(own_half, lax.all_gather(own_half, "row", axis=1, tiled=True))
    return lax.psum_scatter(partial_k, "aux", scatter_dimension=1, tiled=True)


def solution(mesh):
    in_specs = (P("aux", "row", None), P("row", None))
    out_specs = P("row", "aux")
    return jax.shard_map(body, mesh=mesh, in_specs=in_specs, out_specs=out_specs, check_vma=False)
```

profile of v0, /device:TPU:0, one launch (start us, length us, event | category | flops | bytes accessed | tf_op | source)
XLA Modules:
  0.0 642.2 jit_solution(9035648610772449549)
XLA Ops:
  6.5 0.0 all-gather.4.cloned.1.call-start
  6.5 0.7 all-gather.4.cloned.1.call-update
  7.3 0.0 all-gather.6.cloned.1.call-start
  7.3 181.1 %all-gather.4.cloned.1.call-done = bf16[8192,768]{1,0:T(8,128)(2,1)} async-done(((bf16[1024,768]{1,0:T(8,128)(2,1)}), bf16[8192,768]{1,0:T(8,128)(2,1)}) %all-gather.4.cloned.1.call-update) | async-done | bytes 12582928 | tf_op jit(solution)/shard_map/all_gather | solution.py:15
  188.4 19.8 %fusion.2 = bf16[1024,768]{1,0:T(8,128)(2,1)} fusion(bf16[8192,768]{1,0:T(8,128)(2,1)} %all-gather.4.cloned.1.call-done, bf16[1,1024,8192]{2,1,0:T(8,128)(2,1)} %param.2), kind=kOutput, calls=%fused_computation.2 | convolution fusion | flops 12885688320 | bytes 30932992 | tf_op jit(solution)/shard_map/arn,no->aro/dot_general | solution.py:12
  208.2 0.0 all-gather.6.cloned.1.call-update
  208.2 0.0 reduce-scatter.2.cloned.1.call-start
  208.3 174.4 %all-gather.6.cloned.1.call-done = bf16[8192,768]{1,0:T(8,128)(2,1)} async-done(((bf16[1024,768]{1,0:T(8,128)(2,1)}), bf16[8192,768]{1,0:T(8,128)(2,1)}) %all-gather.6.cloned.1.call-update) | async-done | bytes 12582928 | tf_op jit(solution)/shard_map/all_gather | solution.py:19
  382.7 22.4 %fusion.5 = f32[1024,8192]{1,0:T(8,128)} fusion(bf16[1024,768]{1,0:T(8,128)(2,1)} %fusion.2, bf16[8192,768]{1,0:T(8,128)(2,1)} %all-gather.6.cloned.1.call-done), kind=kOutput, calls=%fused_computation.3 | convolution fusion | flops 12884901888 | bytes 47710208 | tf_op jit(solution)/shard_map/aro,aso->rs/dot_general | solution.py:8
  405.1 0.0 reduce-scatter.2.cloned.1.call-update
  405.1 230.6 %reduce-scatter.2.cloned.1.call-done = f32[1024,2048]{1,0:T(8,128)} async-done(((f32[1024,8192]{1,0:T(8,128)}), f32[1024,2048]{1,0:T(8,128)}) %reduce-scatter.2.cloned.1.call-update) | async-done | bytes 8388624 | tf_op jit(solution)/shard_map/reduce_scatter | solution.py:20
Async XLA Ops:
  6.5 181.8 %all-gather.4.cloned.1.call-start = ((), (), s32[]{:S(2)}) async-start(), calls=%async_computation.1 | async-start | bytes 14155776 | tf_op jit(solution)/shard_map/all_gather | solution.py:15
  7.3 375.4 %all-gather.6.cloned.1.call-start = ((), (), s32[]{:S(2)}) async-start(), calls=%async_computation.3 | async-start | bytes 14155776 | tf_op jit(solution)/shard_map/all_gather | solution.py:19
  208.2 427.4 %reduce-scatter.2.cloned.1.call-start = ((), (), s32[]{:S(2)}) async-start(), calls=%async_computation.2 | async-start | bytes 41943040 | tf_op jit(solution)/shard_map/reduce_scatter | solution.py:20
Sparse Core Ops, SparseCore 0:
  9.5 178.8 all-gather.3
  208.3 174.2 all-gather.5
  405.2 230.3 reduce-scatter.1
where the time goes:
time: 642 us
  waiting for transfers between devices  587 us (91%)
  matrix products  42.2 us (7%)
  between operations  13.1 us (2%)
    reduce_scatter x1, waiting for transfers between devices, body(): return lax.psum_scatter(partial_k, 'aux', scatter_dimension=1, tiled=True)  231 us
    all_gather x1, waiting for transfers between devices, body(): lax.all_gather(orbitals, 'row', axis=0, tiled=True)  181 us
    all_gather x1, waiting for transfers between devices, body(): lax.all_gather(own_half, 'row', axis=1, tiled=True)  174 us
    dot_general x1, matrix products, block_product(): jnp.einsum('aro,aso->rs', own_block, other_block, preferred_element_type=...  22.4 us
    dot_general x1, matrix products, body(): jnp.einsum('arn,no->aro', integrals, lax.all_gather(orbitals, 'row', axis...  19.8 us
  transfers between devices with their start and end apart: 3, of which 3 were waited for; matrix products, arithmetic and copies ran while one was open for 0% of the time, Pallas kernels for 0%

commit v1 on v0

v1 whole, which is shorter than its diff:
```python
import jax
import jax.numpy as jnp
from jax import lax
from jax.sharding import PartitionSpec as P


def gather_orbitals(orbitals):
    rows = orbitals.shape[0] // lax.axis_size("aux")
    share = lax.dynamic_slice_in_dim(orbitals, lax.axis_index("aux") * rows, rows, axis=0)
    return lax.all_gather(share, ("row", "aux"), axis=0, tiled=True)


def column_halves(own_half):
    aux, row = lax.axis_size("aux"), lax.axis_size("row")
    span = row // aux
    moves = [
        (p * row + r, (r // span) * row + p * span + r % span)
        for p in range(aux)
        for r in range(row)
    ]
    moved = lax.ppermute(own_half, ("aux", "row"), moves)
    gathered = lax.all_gather(moved, "row", axis=0, tiled=False)
    parts = gathered.reshape((aux, span) + own_half.shape)
    parts = jnp.moveaxis(parts, 2, 1)
    return parts.reshape(aux * own_half.shape[0], span * own_half.shape[1], own_half.shape[2])


def body(integrals, orbitals):
    transformed = jnp.einsum(
        "arn,no->aro",
        integrals,
        gather_orbitals(orbitals),
        preferred_element_type=jnp.float32,
    )
    own_half = transformed.astype(jnp.bfloat16)
    columns = column_halves(own_half)
    rows = lax.all_gather(own_half, "aux", axis=0, tiled=True)
    return jnp.einsum("aro,aco->rc", rows, columns, preferred_element_type=jnp.float32)


def solution(mesh):
    in_specs = (P("aux", "row", None), P("row", None))
    out_specs = P("row", "aux")
    return jax.shard_map(body, mesh=mesh, in_specs=in_specs, out_specs=out_specs, check_vma=False)
```

time: 642 us -> 409 us (0.64)
  waiting for transfers between devices: 587 us -> 342 us
  local copies, waits for them, and re-layouts: 0 us -> 12.5 us
    reduce_scatter x1 -> x0, waiting for transfers between devices: 231 us -> none  [body(): return lax.psum_scatter(partial_k, 'aux', scatter_dimension=1, tiled=True)]
    all_gather x2 -> x3, waiting for transfers between devices: 355 us -> 341 us  [the longest x1 171 us: column_halves(): gathered = lax.all_gather(moved, 'row', axis=0, tiled=False)]
    all_gather x0 -> x1, local copies, waits for them, and re-layouts: none -> 8.71 us  [body(): rows = lax.all_gather(own_half, 'aux', axis=0, tiled=True)]
  transfers between devices with their start and end apart: 3 -> 4, of which waited for: 3 -> 3; matrix products, arithmetic and copies ran while one was open for 0% -> 3% of each run, Pallas kernels for 0% -> 0%
where the time goes in v1:
time: 409 us; the launch traced here: 408 us
  waiting for transfers between devices  342 us (84%)
  matrix products  38.9 us (10%)
  between operations  13.1 us (3%)
  local copies, waits for them, and re-layouts  12.5 us (3%)
    all_gather x1, waiting for transfers between devices, column_halves(): gathered = lax.all_gather(moved, 'row', axis=0, tiled=False)  171 us
    all_gather x1, waiting for transfers between devices, gather_orbitals(): return lax.all_gather(share, ('row', 'aux'), axis=0, tiled=True)  99.3 us
    all_gather x1, waiting for transfers between devices, body(): rows = lax.all_gather(own_half, 'aux', axis=0, tiled=True)  71.2 us
    dot_general x1, matrix products, body(): jnp.einsum('arn,no->aro', integrals, gather_orbitals(orbitals), preferred...  20 us
    dot_general x1, matrix products, body(): jnp.einsum('aro,aco->rc', rows, columns, preferred_element_type=jnp.float32)  19 us
    all_gather x1, local copies, waits for them, and re-layouts, body(): rows = lax.all_gather(own_half, 'aux', axis=0, tiled=True)  8.71 us
  transfers between devices with their start and end apart: 4, of which 3 were waited for; matrix products, arithmetic and copies ran while one was open for 3% of the time, Pallas kernels for 0%

profile of v1, /device:TPU:0, one launch (start us, length us, event | category | flops | bytes accessed | tf_op | source)
XLA Modules:
  0.0 408.2 jit_solution(16350279765923195468)
XLA Ops:
  6.5 0.0 copy-start
  6.5 0.0 all-gather.6.cloned.1.call-start
  6.5 1.4 copy-done
  7.9 0.8 constant_dynamic-slice_fusion
  8.7 0.0 all-gather.6.cloned.1.call-update
  8.7 0.0 all-gather.8.cloned.1.call-start
  8.8 99.3 %all-gather.6.cloned.1.call-done = bf16[8192,768]{1,0:T(8,128)(2,1)} async-done(((bf16[256,768]{1,0:T(8,128)(2,1)}), bf16[8192,768]{1,0:T(8,128)(2,1)}) %all-gather.6.cloned.1.call-update) | async-done | bytes 12582928 | tf_op jit(solution)/shard_map/all_gather | solution.py:10
  108.1 20.0 %fusion.2 = bf16[768,1024]{1,0:T(8,128)(2,1)} fusion(bf16[8192,768]{1,0:T(8,128)(2,1)} %all-gather.6.cloned.1.call-done, bf16[1,1024,8192]{2,1,0:T(8,128)(2,1)} %param.2), kind=kOutput, calls=%fused_computation.3 | convolution fusion | flops 12885688320 | bytes 30932992 | tf_op jit(solution)/shard_map/arn,no->aro/dot_general | solution.py:29
  128.1 0.0 all-gather.8.cloned.1.call-update
  128.1 0.0 all-gather.10.cloned.1.call-start
  128.2 2.1 collective-permute-start
  130.2 0.0 collective-permute-done
  130.2 1.6 copy.6
  131.8 0.0 all-gather.10.cloned.1.call-update
  131.9 71.2 %all-gather.8.cloned.1.call-done = bf16[4096,768]{0,1:T(8,128)(2,1)} async-done(((bf16[1024,768]{0,1:T(8,128)(2,1)}), bf16[4096,768]{0,1:T(8,128)(2,1)}) %all-gather.8.cloned.1.call-update) | async-done | bytes 6291472 | tf_op jit(solution)/shard_map/all_gather | solution.py:37
  203.1 8.7 %copy.8 = bf16[4096,768]{1,0:T(8,128)(2,1)} copy(bf16[4096,768]{0,1:T(8,128)(2,1)} %all-gather.8.cloned.1.call-done) | data formatting | bytes 12582912 | tf_op jit(solution)/shard_map/all_gather | solution.py:37
  211.8 170.9 %all-gather.10.cloned.1.call-done = bf16[8,1024,768]{2,1,0:T(8,128)(2,1)} async-done(((bf16[1,1024,768]{2,1,0:T(8,128)(2,1)}), bf16[8,1024,768]{2,1,0:T(8,128)(2,1)}) %all-gather.10.cloned.1.call-update) | async-done | bytes 12582928 | tf_op jit(solution)/shard_map/all_gather | solution.py:22
  382.7 0.0 copy-start.1
  382.7 19.0 %convolution_bitcast_fusion = f32[1024,2048]{1,0:T(8,128)} fusion(bf16[4,1024,768]{2,1,0:T(8,128)(2,1)} %bitcast.15, bf16[4,2048,768]{2,1,0:T(8,128)(2,1)} %bitcast.18), kind=kOutput, calls=%fused_computation.2 | convolution fusion | flops 12884901888 | bytes 27262976 | tf_op jit(solution)/shard_map/aro,aco->rc/dot_general | solution.py:38
  401.7 0.0 copy-done.1
Async XLA Ops:
  6.5 1.4 copy-start
  6.5 101.6 %all-gather.6.cloned.1.call-start = ((), (), s32[]{:S(2)}) async-start(), calls=%async_computation | async-start | bytes 12976128 | tf_op jit(solution)/shard_map/all_gather | solution.py:10
  8.7 194.3 %all-gather.8.cloned.1.call-start = ((), (), s32[]{:S(2)}) async-start(), calls=%async_computation.1 | async-start | bytes 7864320 | tf_op jit(solution)/shard_map/all_gather | solution.py:37
  128.1 254.6 %all-gather.10.cloned.1.call-start = ((), (), s32[]{:S(2)}) async-start(), calls=%async_computation.2 | async-start | bytes 14155776 | tf_op jit(solution)/shard_map/all_gather | solution.py:22
  128.2 2.1 collective-permute-start
  382.7 19.0 %copy-start.1 = (bf16[1024,768]{1,0:T(8,128)(2,1)S(1)}, bf16[1024,768]{1,0:T(8,128)(2,1)}, u32[]{:S(2)}) copy-start(bf16[1024,768]{1,0:T(8,128)(2,1)} %param.3) | copy-start | bytes 4718596
Sparse Core Ops, SparseCore 0:
  10.2 97.8 all-gather.5
  128.2 74.7 all-gather.7
  205.3 177.3 all-gather.9
